TPU v7x, 256 devices: a whole 4x4x8 slice. The times are simulated.
256 devices in a mesh: expert: 8 (over y_lo, x), rep: 32 (over z, y_hi, core).
Axes of the slice: x: 4, y: 4 (y_hi: 2, y_lo: 2; y = y_hi * 2 + y_lo), z: 8, core: 2. Of those that a mesh axis runs over, the one named last changes fastest.
Arguments:
- route_ids: int32 [2048, 2], P(('expert', 'rep')), may hold values from 0 to 7, all different within a row; in each aligned block of 8 rows (0 to 7, 8 to 15, ...) at most 4 rows name the same one
- route_weight: float32 [2048, 2], P(('expert', 'rep')), may hold values from 0.2 to 0.8
- input_float: bfloat16 [2048, 4096], P(('expert', 'rep')), may hold values from -6 to 6
- input_quant: bfloat16 [2048, 4096], P(('expert', 'rep')), may hold values from -6 to 6
- keep_mask: int32 [2048, 4096], P(('expert', 'rep')), may hold values 0 or 1
- grad_mixed: bfloat16 [2048, 4096], P(('expert', 'rep')), may hold values from -192 to 192
- gate_weight: bfloat16 [8, 4096, 7168], P('expert', None, 'rep'), may hold values from -0.09375 to 0.09375
- up_weight: bfloat16 [8, 4096, 7168], P('expert', None, 'rep'), may hold values from -0.09375 to 0.09375
- down_base: bfloat16 [8, 7168, 4096], P('expert', 'rep'), may hold values from -0.0625 to 0.0625
- down_round: bfloat16 [8, 7168, 4096], P('expert', 'rep'), may hold values from -8 to 8
- down_step: float32 [8, 4096], P('expert'), may hold values from 0.004 to 0.04
Outputs:
- mixed: bfloat16 [2048, 4096], P(('expert', 'rep'))
- round_grad: float32 [8, 7168, 4096], P('expert', 'rep')
Inputs may be any that keep to these rules, and one draw needn't show every extreme that they name: `route_ids`: within the 8 tokens of one device, each expert is named by at most 4 pairs; the two experts of a token differ.
All inputs are finite; a program needn't handle non-finite values. No bound on the sum of `keep_mask` on one device may be relied on, other than what follows from the above.
Results may differ from a plain program's by a relative error of at most 0.0065.
Values may be sent and summed in bfloat16 or wider, within the bound.
No kernel may reach another device: no remote copies, remote signals or barrier semaphores. Data moves between devices by JAX's collectives and lax.ppermute only.
A program may use at most 128 MiB of HBM per device.

v0:
```python
import jax
import jax.numpy as jnp
from jax import lax
from jax.sharding import PartitionSpec as P


def in_one_piece(arrays, axis, split_dim, concat_dim, along):
    both = jnp.concatenate(arrays, axis=along)
    filled, at, gathered = (
        lax.all_to_all(both, axis, split_axis=split_dim, concat_axis=concat_dim, tiled=True),
        0,
        [],
    )
    for a in arrays:
        gathered.append(lax.slice_in_dim(filled, at, at + a.shape[along], axis=along))
        at += a.shape[along]
    return tuple(gathered)


def sent_together(arrays, axis, dim, along):
    ends, at = ([], 0)
    for a in arrays[:-1]:
        at += a.shape[along]
        ends.append(at)
    both = jnp.concatenate(arrays, axis=along)
    return tuple(jnp.split(lax.all_gather(both, axis, axis=dim, tiled=True), ends, axis=along))


def local_slots(route_ids, experts):
    count = route_ids.shape[0]
    flat = route_ids.reshape(count * 2)
    onehot = (flat[:, None] == jnp.arange(experts, dtype=jnp.int32)[None, :]).astype(jnp.int32)
    before = jnp.cumsum(onehot, axis=0) - onehot
    return jnp.sum(before * onehot, axis=1).reshape(count, 2)


def body(
    route_ids,
    route_weight,
    input_float,
    input_quant,
    keep_mask,
    grad_mixed,
    gate_weight,
    up_weight,
    down_base,
    down_round,
    down_step,
):
    experts = lax.axis_size("expert")
    count = route_ids.shape[0]
    capacity = count // 2
    slot = local_slots(route_ids, experts)
    target = route_ids * capacity + slot
    columns = jnp.arange(experts * capacity, dtype=jnp.int32)
    first = (target[:, 0:1] == columns[None, :]).astype(jnp.float32)
    second = (target[:, 1:2] == columns[None, :]).astype(jnp.float32)
    placing = (first + second).astype(jnp.bfloat16)
    weighting = route_weight[:, 0:1] * first + route_weight[:, 1:2] * second
    x_in = jnp.where(keep_mask == 1, input_quant, input_float)
    send_rows = lax.dot_general(
        placing, x_in, (((0,), (0,)), ((), ())), preferred_element_type=jnp.float32
    ).astype(jnp.bfloat16)
    send_cot = lax.dot_general(
        weighting,
        grad_mixed.astype(jnp.float32),
        (((0,), (0,)), ((), ())),
        precision=lax.Precision.HIGHEST,
        preferred_element_type=jnp.float32,
    ).astype(jnp.bfloat16)
    own_rows, own_cot = in_one_piece((send_rows, send_cot), "expert", 0, 0, 1)
    w_gate = gate_weight[0]
    w_up = up_weight[0]
    soft = jax.nn.sigmoid(down_round[0].astype(jnp.float32))
    step_row = down_step[0][None, :]
    quant_down = (down_base[0].astype(jnp.float32) + step_row * soft).astype(jnp.bfloat16)
    all_rows, all_cot = sent_together((own_rows, own_cot), "rep", 0, 1)
    gate = jnp.dot(all_rows, w_gate, preferred_element_type=jnp.float32)
    up = jnp.dot(all_rows, w_up, preferred_element_type=jnp.float32)
    hidden = (jax.nn.silu(gate) * up).astype(jnp.bfloat16)
    grad_w = lax.dot_general(
        hidden, all_cot, (((0,), (0,)), ((), ())), preferred_element_type=jnp.float32
    )
    wide_down = lax.all_to_all(quant_down, "rep", split_axis=1, concat_axis=0, tiled=True)
    out_cols = jnp.dot(
        lax.all_gather(hidden, "rep", axis=1, tiled=True),
        wide_down,
        preferred_element_type=jnp.float32,
    )
    summed = lax.all_to_all(
        out_cols.astype(jnp.bfloat16), "rep", split_axis=0, concat_axis=1, tiled=True
    )
    returned = lax.all_to_all(summed, "expert", split_axis=0, concat_axis=0, tiled=True)
    mixed = jnp.dot(
        weighting,
        returned.astype(jnp.float32),
        precision=lax.Precision.HIGHEST,
        preferred_element_type=jnp.float32,
    ).astype(jnp.bfloat16)
    round_grad = (grad_w * step_row * soft * (1.0 - soft))[None]
    return (mixed, round_grad)


def solution(mesh):
    return jax.shard_map(
        body,
        mesh=mesh,
        in_specs=(
            P(("expert", "rep"), None),
            P(("expert", "rep"), None),
            P(("expert", "rep"), None),
            P(("expert", "rep"), None),
            P(("expert", "rep"), None),
            P(("expert", "rep"), None),
            P("expert", None, "rep"),
            P("expert", None, "rep"),
            P("expert", "rep", None),
            P("expert", "rep", None),
            P("expert", None),
        ),
        out_specs=(P(("expert", "rep"), None), P("expert", "rep", None)),
        check_vma=False,
    )
```

profile of v0, /device:TPU:1, one launch (start us, length us, event | category | flops | bytes accessed | tf_op | source)
XLA Modules:
  0.0 381.1 jit_solution(1803155560595772534)
XLA Ops:
  7.2 0.8 slice_bitcast_fusion.1
  8.1 0.8 copy.23
  8.8 0.1 eq.51
  9.0 0.2 select_reduce_fusion
  9.2 0.1 reshape.38
  9.3 0.2 slice_reduce_fusion.1
  9.5 1.3 convolution_convert_fusion.1
  10.8 1.3 convolution_convert_fusion
  12.1 0.2 all_to_all.40
  12.3 14.9 %all_to_all.56 = bf16[8,4,8192]{2,1,0:T(4,128)(2,1)S(1)} all-to-all(bf16[8,4,8192]{2,1,0:T(4,128)(2,1)S(1)} %all_to_all.40), channel_id=1, replica_groups=mesh['expert'=8,'rep'=32] {'expert'}, dimensions={0} | all-to-all | bytes 1048576 | tf_op jit(solution)/shard_map/all_to_all | solution.py:10
  27.2 0.9 all_to_all.42
  28.2 139.6 %all-gather.3.cloned.1.call-done = bf16[1024,8192]{1,0:T(8,128)(2,1)} async-done(((bf16[32,8192]{1,0:T(8,128)(2,1)}), bf16[1024,8192]{1,0:T(8,128)(2,1)}) %all-gather.3.cloned.1.call-update) | async-done | bytes 16777232 | tf_op jit(solution)/shard_map/all_gather | solution.py:26
  167.8 6.1 %fusion.4 = f32[1024,224]{0,1:T(8,128)S(1)} fusion(bf16[1024,8192]{1,0:T(8,128)(2,1)} %all-gather.3.cloned.1.call-done, bf16[1,4096,224]{1,2,0:T(8,128)(2,1)S(1)} %copy-done), kind=kOutput, calls=%fused_computation.4 | convolution fusion | flops 1879048192 | bytes 11141120 | tf_op jit(solution)/shard_map/dot_general | solution.py:78
  174.0 2.0 copy-done.6
  176.0 0.5 copy-done.7
  176.5 3.5 fusion.28
  180.0 0.4 convert_bitcast_fusion
  180.5 0.6 copy.27
  181.1 0.8 copy-done.3
  182.0 1.0 fusion.22
  182.9 0.6 copy.28
  183.6 0.9 fusion.19
  184.6 0.7 copy.25
  185.3 67.5 %all_to_all.57 = bf16[224,32,128]{2,0,1:T(8,128)(2,1)S(1)} all-to-all(bf16[224,32,128]{2,0,1:T(8,128)(2,1)S(1)} %copy.25), channel_id=1, replica_groups=mesh['expert'=8,'rep'=32] {'rep'}, dimensions={1} | all-to-all | bytes 3670016 | tf_op jit(solution)/shard_map/all_to_all | solution.py:84
  252.8 81.7 %all-gather.5.cloned.1.call-done = bf16[1024,7168]{0,1:T(8,128)(2,1)} async-done(((bf16[1024,224]{0,1:T(8,128)(2,1)}), bf16[1024,7168]{0,1:T(8,128)(2,1)}) %all-gather.5.cloned.1.call-update) | async-done | bytes 14680080 | tf_op jit(solution)/shard_map/all_gather | solution.py:86
  334.5 7.3 %convolution_convert_fusion.3 = bf16[1024,128]{1,0:T(8,128)(2,1)S(1)} fusion(bf16[1024,7168]{0,1:T(8,128)(2,1)} %all-gather.5.cloned.1.call-done, bf16[7168,128]{1,0:T(8,128)(2,1)S(1)} %bitcast.47), kind=kOutput, calls=%fused_computation.24 | convolution fusion | flops 1879179264 | bytes 16777216 | tf_op jit(solution)/shard_map/dot_general | solution.py:85
  341.9 17.4 %all_to_all.58 = bf16[32,32,128]{2,1,0:T(8,128)(2,1)S(1)} all-to-all(bf16[32,32,128]{2,1,0:T(8,128)(2,1)S(1)} %bitcast.49), channel_id=1, replica_groups=mesh['expert'=8,'rep'=32] {'rep'}, dimensions={0} | all-to-all | bytes 524288 | tf_op jit(solution)/shard_map/all_to_all | solution.py:90
  359.3 0.1 copy.26
  359.4 0.8 all_to_all.49
  360.2 4.8 %all-to-all-start.3 = ((bf16[8,4,4096]{2,1,0:T(4,128)(2,1)}), bf16[8,4,4096]{2,1,0:T(4,128)(2,1)S(1)}, u32[]{:S(2)}, u32[]{:S(2)}) async-start(bf16[8,4,4096]{2,1,0:T(4,128)(2,1)} %all_to_all.49), calls=%async_computation.3 | async-start | bytes 524288 | tf_op jit(solution)/shard_map/all_to_all | solution.py:93
  365.1 8.2 %fusion.15 = f32[1,224,4096]{2,1,0:T(8,128)} fusion(bf16[1024,224]{0,1:T(8,128)(2,1)S(1)} %copy-done.4, bf16[1024,8192]{1,0:T(8,128)(2,1)} %all-gather.3.cloned.1.call-done, f32[4096]{0:T(1024)S(1)} %bitcast.51, bf16[1,224,4096]{2,1,0:T(8,128)(2,1)} %param.20), kind=kOutput, calls=%fused_computation.9 | convolution fusion | flops 1886388224 | bytes 14368768 | tf_op jit(solution)/shard_map/dot_general | solution.py:81
  373.3 0.9 convolution_convert_fusion.2
  (23 shorter events, 0.4 us)
Async XLA Ops:
  7.2 160.7 %copy-start = (bf16[1,4096,224]{1,2,0:T(8,128)(2,1)S(1)}, bf16[1,4096,224]{1,2,0:T(8,128)(2,1)}, u32[]{:S(2)}) copy-start(bf16[1,4096,224]{1,2,0:T(8,128)(2,1)} %param.17) | copy-start | bytes 5505028
  7.2 160.6 %all-gather.3.cloned.1.call-start = ((), (), s32[]{:S(2)}) async-start(), calls=%async_computation.4 | async-start | bytes 17301504 | tf_op jit(solution)/shard_map/all_gather | solution.py:26
  28.2 306.3 %all-gather.5.cloned.1.call-start = ((), (), s32[]{:S(2)}) async-start(), calls=%async_computation.5 | async-start | bytes 15138816 | tf_op jit(solution)/shard_map/all_gather | solution.py:86
  167.8 8.2 %copy-start.6 = (bf16[1024,8192]{1,0:T(8,128)(2,1)S(1)}, bf16[1024,8192]{1,0:T(8,128)(2,1)}, u32[]{:S(2)}) copy-start(bf16[1024,8192]{1,0:T(8,128)(2,1)} %all-gather.3.cloned.1.call-done) | copy-start | bytes 50331652
  167.8 8.7 %copy-start.7 = (bf16[1,4096,224]{1,2,0:T(8,128)(2,1)S(1)}, bf16[1,4096,224]{1,2,0:T(8,128)(2,1)}, u32[]{:S(2)}) copy-start(bf16[1,4096,224]{1,2,0:T(8,128)(2,1)} %param.18) | copy-start | bytes 5505028
  176.5 3.6 copy-start.2
  180.5 1.5 copy-start.3
  182.9 0.7 copy-start.5
  334.5 30.5 %copy-start.4 = (bf16[1024,224]{0,1:T(8,128)(2,1)S(1)}, bf16[1024,224]{0,1:T(8,128)(2,1)}, u32[]{:S(2)}) copy-start(bf16[1024,224]{0,1:T(8,128)(2,1)} %fusion.28) | copy-start | bytes 1376260
  360.2 13.1 %all-to-all-start.3 = ((bf16[8,4,4096]{2,1,0:T(4,128)(2,1)}), bf16[8,4,4096]{2,1,0:T(4,128)(2,1)S(1)}, u32[]{:S(2)}, u32[]{:S(2)}) async-start(bf16[8,4,4096]{2,1,0:T(4,128)(2,1)} %all_to_all.49), calls=%async_computation.3 | async-start | bytes 524288 | tf_op jit(solution)/shard_map/all_to_all | solution.py:93
  365.0 9.2 %copy-start.1 = (bf16[1,4096,224]{1,2,0:T(8,128)(2,1)S(1)}, bf16[1,4096,224]{1,2,0:T(8,128)(2,1)}, u32[]{:S(2)}) copy-start(bf16[1,4096,224]{1,2,0:T(8,128)(2,1)} %param.17) | copy-start | bytes 5505028
Sparse Core Ops, SparseCore 0:
  28.3 139.4 all-gather.2
  180.2 154.3 all-gather.4
where the time goes:
time: 382 us; the launch traced here: 381 us
  waiting for transfers between devices  221 us (58%)
  blocking collectives  99.8 us (26%)
  matrix products  28.8 us (8%)
  between operations  14.2 us (4%)
  local copies, waits for them, and re-layouts  9.41 us (2%)
  starting transfers between devices  4.93 us (1%)
    all_gather x1, waiting for transfers between devices, sent_together(): lax.all_gather(both, axis, axis=dim, tiled=True)  140 us
    all_gather x1, waiting for transfers between devices, body(): lax.all_gather(hidden, 'rep', axis=1, tiled=True)  81.7 us
    all_to_all x1, blocking collectives, body(): lax.all_to_all(quant_down, 'rep', split_axis=1, concat_axis=0, tiled=True)  67.5 us
    all_to_all x1, blocking collectives, body(): lax.all_to_all(out_cols.astype(jnp.bfloat16), 'rep', split_axis=0, concat...  17.4 us
    all_to_all x1, blocking collectives, in_one_piece(): lax.all_to_all(both, axis, split_axis=split_dim, concat_axis=concat_dim,...  14.9 us
    dot_general x1, matrix products, body(): lax.dot_general(hidden, all_cot, (((0,), (0,)), ((), ())), preferred_elem...  8.21 us
  transfers between devices with their start and end apart: 3, of which 2 were waited for; matrix products, arithmetic and copies ran while one was open for 3% of the time, Pallas kernels for 0%

commit v1 on v0

--- a/solution.py
+++ b/solution.py
@@ -2,6 +2,13 @@
 import jax.numpy as jnp
 from jax import lax
 from jax.sharding import PartitionSpec as P
+
+
+def gather_over(x, name, dim):
+    peers = lax.axis_size(name)
+    tiles = jnp.stack([x for _ in range(peers)])
+    tiles = lax.all_to_all(tiles, name, split_axis=0, concat_axis=0)
+    return jnp.concatenate(tiles, axis=dim)
 
 
 def in_one_piece(arrays, axis, split_dim, concat_dim, along):
@@ -82,11 +89,7 @@
         hidden, all_cot, (((0,), (0,)), ((), ())), preferred_element_type=jnp.float32
     )
     wide_down = lax.all_to_all(quant_down, "rep", split_axis=1, concat_axis=0, tiled=True)
-    out_cols = jnp.dot(
-        lax.all_gather(hidden, "rep", axis=1, tiled=True),
-        wide_down,
-        preferred_element_type=jnp.float32,
-    )
+    out_cols = jnp.dot(gather_over(hidden, "rep", 1), wide_down, preferred_element_type=jnp.float32)
     summed = lax.all_to_all(
         out_cols.astype(jnp.bfloat16), "rep", split_axis=0, concat_axis=1, tiled=True
     )

time: 382 us -> 592 us (1.55)
  blocking collectives: 99.8 us -> 358 us
  waiting for transfers between devices: 221 us -> 150 us
  starting transfers between devices: 4.93 us -> 17.7 us
  local copies, waits for them, and re-layouts: 9.41 us -> 15.8 us
  other arithmetic: 2.61 us -> 8.68 us
    all_to_all x1, blocking collectives: 67.5 us -> 325 us  [gather_over(): tiles = lax.all_to_all(tiles, name, split_axis=0, concat_axis=0)]
    all_gather x1 -> x0, waiting for transfers between devices: 81.7 us -> none  [body(): lax.all_gather(hidden, 'rep', axis=1, tiled=True)]
    all_to_all x0 -> x1, starting transfers between devices: none -> 12.8 us  [body(): lax.all_to_all(quant_down, 'rep', split_axis=1, concat_axis=0, tiled=True)]
    all_gather x1, waiting for transfers between devices: 140 us -> 150 us  [sent_together(): lax.all_gather(both, axis, axis=dim, tiled=True)]
    another operation x0 -> x1, local copies, waits for them, and re-layouts: none -> 7.08 us  [gather_over(): tiles = jnp.stack([x for _ in range(peers)])]
  transfers between devices with their start and end apart: 3 -> 3, of which waited for: 2 -> 1; matrix products, arithmetic and copies ran while one was open for 3% -> 5% of each run, Pallas kernels for 0% -> 0%
where the time goes in v1:
time: 592 us; the launch traced here: 591 us
  blocking collectives  358 us (60%)
  waiting for transfers between devices  150 us (25%)
  matrix products  26.2 us (4%)
  starting transfers between devices  17.7 us (3%)
  local copies, waits for them, and re-layouts  15.8 us (3%)
  between operations  14.2 us (2%)
  other arithmetic  8.68 us (1%)
    all_to_all x1, blocking collectives, gather_over(): tiles = lax.all_to_all(tiles, name, split_axis=0, concat_axis=0)  325 us
    all_gather x1, waiting for transfers between devices, sent_together(): lax.all_gather(both, axis, axis=dim, tiled=True)  150 us
    all_to_all x1, blocking collectives, body(): lax.all_to_all(out_cols.astype(jnp.bfloat16), 'rep', split_axis=0, concat...  18.6 us
    all_to_all x1, blocking collectives, in_one_piece(): lax.all_to_all(both, axis, split_axis=split_dim, concat_axis=concat_dim,...  14.9 us
    all_to_all x1, starting transfers between devices, body(): lax.all_to_all(quant_down, 'rep', split_axis=1, concat_axis=0, tiled=True)  12.8 us
  transfers between devices with their start and end apart: 3, of which 1 were waited for; matrix products, arithmetic and copies ran while one was open for 5% of the time, Pallas kernels for 0%

profile of v1, /device:TPU:1, one launch (start us, length us, event | category | flops | bytes accessed | tf_op | source)
XLA Modules:
  0.0 591.0 jit_solution(10759255446533942004)
XLA Ops:
  7.2 0.8 slice_bitcast_fusion.1
  8.1 0.8 copy.20
  8.8 0.1 eq.51
  9.0 0.2 select_reduce_fusion
  9.2 0.1 reshape.44
  9.3 0.2 slice_reduce_fusion.1
  9.5 1.3 convolution_convert_fusion.1
  10.8 1.3 convolution_convert_fusion
  12.1 0.2 all_to_all.41
  12.3 14.9 %all_to_all.58 = bf16[8,4,8192]{2,1,0:T(4,128)(2,1)S(1)} all-to-all(bf16[8,4,8192]{2,1,0:T(4,128)(2,1)S(1)} %all_to_all.41), channel_id=1, replica_groups=mesh['expert'=8,'rep'=32] {'expert'}, dimensions={0} | all-to-all | bytes 1048576 | tf_op jit(solution)/shard_map/all_to_all | solution.py:17
  27.2 0.9 all_to_all.43
  28.2 1.9 convert_bitcast_fusion
  30.1 0.6 copy.25
  30.7 0.8 copy-done.2
  31.6 1.0 fusion.24
  32.6 0.6 copy.26
  33.3 5.5 fusion.20
  38.7 12.8 %all-to-all-start.2 = ((bf16[224,32,128]{2,0,1:T(8,128)(2,1)}), bf16[224,32,128]{2,0,1:T(8,128)(2,1)}, u32[]{:S(2)}, u32[]{:S(2)}) async-start(bf16[224,32,128]{2,0,1:T(8,128)(2,1)} %fusion.20), calls=%async_computation.2 | async-start | bytes 3670016 | tf_op jit(solution)/shard_map/all_to_all | solution.py:91
  51.6 150.1 %all-gather.2.cloned.1.call-done = bf16[1024,8192]{1,0:T(8,128)(2,1)} async-done(((bf16[32,8192]{1,0:T(8,128)(2,1)}), bf16[1024,8192]{1,0:T(8,128)(2,1)}) %all-gather.2.cloned.1.call-update) | async-done | bytes 16777232 | tf_op jit(solution)/shard_map/all_gather | solution.py:33
  201.7 6.1 %fusion.6 = f32[1024,224]{0,1:T(8,128)S(1)} fusion(bf16[1024,8192]{1,0:T(8,128)(2,1)} %all-gather.2.cloned.1.call-done, bf16[1,4096,224]{1,2,0:T(8,128)(2,1)S(1)} %copy-done), kind=kOutput, calls=%fused_computation.6 | convolution fusion | flops 1879048192 | bytes 11141120 | tf_op jit(solution)/shard_map/dot_general | solution.py:85
  207.8 2.0 copy-done.4
  209.8 0.5 copy-done.5
  210.3 2.7 fusion.30
  213.1 7.1 %stack.2 = bf16[32,1024,224]{1,2,0:T(8,128)(2,1)} broadcast(bf16[1024,224]{0,1:T(8,128)(2,1)S(1)} %fusion.30), dimensions={1,2} | broadcast | bytes 15138816 | tf_op jit(solution)/shard_map/stack | solution.py:9
  220.1 324.9 %all_to_all.59 = bf16[32,1024,224]{1,2,0:T(8,128)(2,1)S(1)} all-to-all(bf16[32,1024,224]{1,2,0:T(8,128)(2,1)} %stack.2), channel_id=1, replica_groups=mesh['expert'=8,'rep'=32] {'rep'}, dimensions={0} | all-to-all | bytes 29360128 | tf_op jit(solution)/shard_map/all_to_all | solution.py:10
  545.0 5.6 fusion.40
  550.6 18.6 %all_to_all.60 = bf16[32,32,128]{2,1,0:T(8,128)(2,1)S(1)} all-to-all(bf16[32,32,128]{2,1,0:T(8,128)(2,1)S(1)} %bitcast.57), channel_id=1, replica_groups=mesh['expert'=8,'rep'=32] {'rep'}, dimensions={0} | all-to-all | bytes 524288 | tf_op jit(solution)/shard_map/all_to_all | solution.py:93
  569.2 0.1 copy.24
  569.3 0.8 all_to_all.50
  570.1 4.9 all-to-all-start.4
  574.9 8.2 %fusion.17 = f32[1,224,4096]{2,1,0:T(8,128)} fusion(bf16[1024,224]{0,1:T(8,128)(2,1)S(1)} %fusion.30, bf16[1024,8192]{1,0:T(8,128)(2,1)} %all-gather.2.cloned.1.call-done, f32[4096]{0:T(1024)S(1)} %bitcast.59, bf16[1,224,4096]{2,1,0:T(8,128)(2,1)} %param.20), kind=kOutput, calls=%fused_computation.11 | convolution fusion | flops 1886388224 | bytes 14368768 | tf_op jit(solution)/shard_map/dot_general | solution.py:88
  583.2 0.9 convolution_convert_fusion.2
  (18 shorter events, 0.4 us)
Async XLA Ops:
  7.2 194.5 %copy-start = (bf16[1,4096,224]{1,2,0:T(8,128)(2,1)S(1)}, bf16[1,4096,224]{1,2,0:T(8,128)(2,1)}, u32[]{:S(2)}) copy-start(bf16[1,4096,224]{1,2,0:T(8,128)(2,1)} %param.17) | copy-start | bytes 5505028
  7.2 194.5 %all-gather.2.cloned.1.call-start = ((), (), s32[]{:S(2)}) async-start(), calls=%async_computation.5 | async-start | bytes 17301504 | tf_op jit(solution)/shard_map/all_gather | solution.py:33
  30.1 1.5 copy-start.2
  32.5 0.7 copy-start.3
  38.7 174.3 %all-to-all-start.2 = ((bf16[224,32,128]{2,0,1:T(8,128)(2,1)}), bf16[224,32,128]{2,0,1:T(8,128)(2,1)}, u32[]{:S(2)}, u32[]{:S(2)}) async-start(bf16[224,32,128]{2,0,1:T(8,128)(2,1)} %fusion.20), calls=%async_computation.2 | async-start | bytes 3670016 | tf_op jit(solution)/shard_map/all_to_all | solution.py:91
  201.7 8.2 %copy-start.4 = (bf16[1024,8192]{1,0:T(8,128)(2,1)S(1)}, bf16[1024,8192]{1,0:T(8,128)(2,1)}, u32[]{:S(2)}) copy-start(bf16[1024,8192]{1,0:T(8,128)(2,1)} %all-gather.2.cloned.1.call-done) | copy-start | bytes 50331652
  201.7 8.7 %copy-start.5 = (bf16[1,4096,224]{1,2,0:T(8,128)(2,1)S(1)}, bf16[1,4096,224]{1,2,0:T(8,128)(2,1)}, u32[]{:S(2)}) copy-start(bf16[1,4096,224]{1,2,0:T(8,128)(2,1)} %param.18) | copy-start | bytes 5505028
  570.1 13.1 %all-to-all-start.4 = ((bf16[8,4,4096]{2,1,0:T(4,128)(2,1)}), bf16[8,4,4096]{2,1,0:T(4,128)(2,1)S(1)}, u32[]{:S(2)}, u32[]{:S(2)}) async-start(bf16[8,4,4096]{2,1,0:T(4,128)(2,1)} %all_to_all.50), calls=%async_computation.4 | async-start | bytes 524288 | tf_op jit(solution)/shard_map/all_to_all | solution.py:96
  574.9 9.2 %copy-start.1 = (bf16[1,4096,224]{1,2,0:T(8,128)(2,1)S(1)}, bf16[1,4096,224]{1,2,0:T(8,128)(2,1)}, u32[]{:S(2)}) copy-start(bf16[1,4096,224]{1,2,0:T(8,128)(2,1)} %param.17) | copy-start | bytes 5505028
Sparse Core Ops, SparseCore 0:
  28.3 173.3 all-gather.1
